TPU v7x, 32 devices: a whole 2x2x4 slice. The times are simulated.
32 devices in a mesh: ens: 2 (over y), gx: 4 (over z), col: 2 (over x), gz: 2 (over core).
Axes of the slice: x: 2, y: 2, z: 4, core: 2. Of those that a mesh axis runs over, the one named last changes fastest.
Arguments:
- checkpoints: bfloat16 [8, 3, 32, 8, 256], P(('ens', 'col'), None, 'gz', 'gx'), parts along dimension 0, may hold values from -3 to 3
- obs_values: float32 [8, 32, 8, 256], P('ens', 'gz', 'gx', 'col'), parts along dimension 0, may hold values from -3 to 3
- obs_mask: int32 [8, 32, 8, 256], P('ens', 'gz', 'gx', 'col'), parts along dimension 0, may hold values 0 or 1
- drag: float32 [64], P(('ens', 'gz')), parts along dimension 0, may hold values from 0.05 to 0.5
Outputs:
- grad_init: float32 [6, 32, 8, 256], P('ens', 'gz', 'gx', 'col'), parts along dimension 0
- cost_levels: float32 [64], P(('ens', 'gz')), parts along dimension 0
- drag_grad: float32 [64], P(('ens', 'gz')), parts along dimension 0
There are 2 independent parts, one for each index of `ens`. A program takes and returns all parts, laid end to end along the dimension named above; each array names one. Nothing has to cross between parts.
All inputs are finite; a program needn't handle non-finite values. No bound on the sum of `obs_mask` on one device may be relied on, other than what follows from the above.
Results may differ from a plain program's by a relative error of at most 0.0003.
Values may be sent and summed in bfloat16 or wider, within the bound.
A program may use at most 64 MiB of HBM per device.

v0:
```python
import jax
import jax.numpy as jnp
from jax import lax
from jax.sharding import PartitionSpec as P

SEG = 2
time_step = 0.1
viscosity = 0.05
vertical_mix = 0.2


def with_halo(x, sides, width):
    for axis, dim in sides:
        devices, length = (lax.axis_size(axis), x.shape[dim])
        up = [(i, (i + 1) % devices) for i in range(devices - 1)]
        down = [(j, i) for i, j in up]
        last = lax.slice_in_dim(x, length - width, length, axis=dim)
        initial = lax.slice_in_dim(x, 0, width, axis=dim)
        before = lax.ppermute(last, axis, up)
        after = lax.ppermute(initial, axis, down)
        x = jnp.concatenate([before, x, after], axis=dim)
    return x


def passed_along(block, axis, distance):
    devices = range(lax.axis_size(axis))
    route = [(i - distance, i) for i in devices if i - distance in devices]
    return lax.ppermute(block, axis, route)


def along_cols(a):
    return 0.5 * (a[:, 1:-1, 2:] - a[:, 1:-1, :-2])


def along_rows(a):
    return 0.5 * (a[:, 2:, 1:-1] - a[:, :-2, 1:-1])


def laplace(a):
    return (
        a[:, 2:, 1:-1] + a[:, :-2, 1:-1] + a[:, 1:-1, 2:] + a[:, 1:-1, :-2] - 4.0 * a[:, 1:-1, 1:-1]
    )


def advance(padded, drag, coriolis):
    levels = padded[:, 1:-1]
    thick, zonal, merid = (levels[0], levels[1], levels[2])
    centre = padded[:, 1:-1, 1:-1, 1:-1]
    h_c, u_c, v_c = (centre[0], centre[1], centre[2])
    rot = coriolis[None, :, None]
    rate = drag[:, None, None]
    vert = padded[:, 2:, 1:-1, 1:-1] + padded[:, :-2, 1:-1, 1:-1] - 2.0 * centre
    u_new = (
        u_c
        + time_step
        * (
            -along_cols(thick)
            - u_c * along_cols(zonal)
            - v_c * along_rows(zonal)
            + rot * v_c
            - rate * u_c
        )
        + viscosity * laplace(zonal)
    )
    v_new = (
        v_c
        + time_step
        * (
            -along_rows(thick)
            - u_c * along_cols(merid)
            - v_c * along_rows(merid)
            - rot * u_c
            - rate * v_c
        )
        + viscosity * laplace(merid)
    )
    h_new = (
        h_c
        - time_step
        * (
            along_cols(zonal)
            + along_rows(merid)
            + along_cols(thick * zonal)
            + along_rows(thick * merid)
        )
        + viscosity * laplace(thick)
    )
    return jnp.stack([h_new, u_new, v_new]) + vertical_mix * vert


def extend(state):
    return with_halo(state, (("gx", 2), ("col", 3), ("gz", 1)), 1)


def halo_back(cot):
    inner = cot[:, 1:-1, 1:-1, 1:-1]
    below = passed_along(cot[:, 0, 1:-1, 1:-1], "gz", -1)
    above = passed_along(cot[:, -1, 1:-1, 1:-1], "gz", 1)
    inner = inner.at[:, -1].add(below).at[:, 0].add(above)
    south = passed_along(cot[:, 1:-1, 0, 1:-1], "gx", -1)
    north = passed_along(cot[:, 1:-1, -1, 1:-1], "gx", 1)
    inner = inner.at[:, :, -1].add(south).at[:, :, 0].add(north)
    west = passed_along(cot[:, 1:-1, 1:-1, 0], "col", -1)
    east = passed_along(cot[:, 1:-1, 1:-1, -1], "col", 1)
    return inner.at[:, :, :, -1].add(west).at[:, :, :, 0].add(east)


def on_device(checkpoints, obs_values, obs_mask, drag):
    lat_count = obs_values.shape[2]
    lon_count = obs_values.shape[3]
    segments = obs_values.shape[0]
    total_lat = lat_count * lax.axis_size("gx")
    total_lon = lon_count * lax.axis_size("col")
    rows = (lax.axis_index("gx") * lat_count + jnp.arange(lat_count)).astype(jnp.float32)
    cols = (lax.axis_index("col") * lon_count + jnp.arange(lon_count)).astype(jnp.float32)
    coriolis = 0.2 + 0.1 * rows / total_lat
    weight = (1.0 + 2.0 * rows / total_lat)[:, None] * (1.0 + 2.0 * cols / total_lon)[None, :]
    owned_cols = lax.all_to_all(checkpoints, "col", split_axis=4, concat_axis=0, tiled=True)

    def local(padded, rate):
        return advance(padded, rate, coriolis)

    levels = drag.shape[0]
    adjoint = jnp.zeros((3, levels, lat_count, lon_count), jnp.float32)
    cost = jnp.zeros((levels,), jnp.float32)
    drag_total = jnp.zeros((levels,), jnp.float32)
    for seg in reversed(range(segments)):
        state = owned_cols[seg].astype(jnp.float32)
        pads = []
        for step in range(SEG):
            padded = extend(state)
            pads.append(padded)
            state = advance(padded, drag, coriolis)
        resid = state[0] - obs_values[seg]
        forcing = weight[None] * obs_mask[seg].astype(jnp.float32) * resid
        seg_cost = 0.5 * jnp.sum(forcing * resid, axis=(1, 2))
        adjoint = adjoint.at[0].add(forcing)
        seg_drag = jnp.zeros((levels,), jnp.float32)
        for step in reversed(range(SEG)):
            unused, pull = jax.vjp(local, pads[step], drag)
            cot_pad, cot_drag = pull(adjoint)
            seg_drag = seg_drag + cot_drag
            adjoint = halo_back(cot_pad)
        summed_drag, summed_cost = lax.psum((seg_drag, seg_cost), ("gx", "col"))
        drag_total = drag_total + summed_drag
        cost = cost + summed_cost
    scale = 1.0 / (total_lat * total_lon)
    return (adjoint, cost * scale, drag_total * scale)


def solution(mesh):
    return jax.shard_map(
        on_device,
        mesh=mesh,
        in_specs=(
            P(("ens", "col"), None, "gz", "gx", None),
            P("ens", "gz", "gx", "col"),
            P("ens", "gz", "gx", "col"),
            P(("ens", "gz")),
        ),
        out_specs=(P("ens", "gz", "gx", "col"), P(("ens", "gz")), P(("ens", "gz"))),
        check_vma=False,
    )
```

profile of v0, /device:TPU:0, one launch (start us, length us, event | category | flops | bytes accessed | tf_op | source)
XLA Modules:
  0.0 335.3 jit_solution(2285676061232083874)
XLA Ops:
  20.0 4.5 %collective-permute-start.24 = (f32[3,16,1,128]{3,1,2,0:T(8,128)S(1)}, f32[3,16,1,128]{3,1,2,0:T(8,128)S(1)}, u32[]{:S(2)}, u32[]{:S(2)}) collective-permute-start(f32[3,16,1,128]{3,1,2,0:T(8,128)S(1)} %get-tuple-element.1057), channel_id=1, source_target_pairs={{0,4},{4,8},{8,12},{1,5},{5,9},{9,13},{2,6},{6,10},{10,14},{3,7},{... | collective-permute-start | bytes 73736 | tf_op jit(solution)/shard_map/ppermute | solution.py:19
  25.9 4.5 %collective-permute-start.48 = (f32[3,16,1,128]{3,1,2,0:T(8,128)S(1)}, f32[3,16,1,128]{3,1,2,0:T(8,128)S(1)}, u32[]{:S(2)}, u32[]{:S(2)}) collective-permute-start(f32[3,16,1,128]{3,1,2,0:T(8,128)S(1)} %get-tuple-element.1061), channel_id=1, source_target_pairs={{0,4},{4,8},{8,12},{1,5},{5,9},{9,13},{2,6},{6,10},{10,14},{3,7},{... | collective-permute-start | bytes 73736 | tf_op jit(solution)/shard_map/ppermute | solution.py:19
  31.8 4.5 %collective-permute-start.72 = (f32[3,16,1,128]{3,1,2,0:T(8,128)S(1)}, f32[3,16,1,128]{3,1,2,0:T(8,128)S(1)}, u32[]{:S(2)}, u32[]{:S(2)}) collective-permute-start(f32[3,16,1,128]{3,1,2,0:T(8,128)S(1)} %get-tuple-element.1065), channel_id=1, source_target_pairs={{0,4},{4,8},{8,12},{1,5},{5,9},{9,13},{2,6},{6,10},{10,14},{3,7},{... | collective-permute-start | bytes 73736 | tf_op jit(solution)/shard_map/ppermute | solution.py:19
  41.1 4.6 %collective-permute-start.26 = (f32[3,16,4,1]{3,1,2,0:T(8,128)S(1)}, f32[3,16,4,1]{3,1,2,0:T(8,128)S(1)}, u32[]{:S(2)}, u32[]{:S(2)}) collective-permute-start(f32[3,16,4,1]{3,1,2,0:T(8,128)S(1)} %get-tuple-element.948), channel_id=1, source_target_pairs={{0,2},{1,3},{4,6},{5,7},{8,10},{9,11},{12,14},{13,15},{16,18},{17,... | collective-permute-start | bytes 2312 | tf_op jit(solution)/shard_map/ppermute | solution.py:19
  47.1 4.6 %collective-permute-start.50 = (f32[3,16,4,1]{3,1,2,0:T(8,128)S(1)}, f32[3,16,4,1]{3,1,2,0:T(8,128)S(1)}, u32[]{:S(2)}, u32[]{:S(2)}) collective-permute-start(f32[3,16,4,1]{3,1,2,0:T(8,128)S(1)} %get-tuple-element.952), channel_id=1, source_target_pairs={{0,2},{1,3},{4,6},{5,7},{8,10},{9,11},{12,14},{13,15},{16,18},{17,... | collective-permute-start | bytes 2312 | tf_op jit(solution)/shard_map/ppermute | solution.py:19
  53.1 4.6 %collective-permute-start.74 = (f32[3,16,4,1]{3,1,2,0:T(8,128)S(1)}, f32[3,16,4,1]{3,1,2,0:T(8,128)S(1)}, u32[]{:S(2)}, u32[]{:S(2)}) collective-permute-start(f32[3,16,4,1]{3,1,2,0:T(8,128)S(1)} %get-tuple-element.956), channel_id=1, source_target_pairs={{0,2},{1,3},{4,6},{5,7},{8,10},{9,11},{12,14},{13,15},{16,18},{17,... | collective-permute-start | bytes 2312 | tf_op jit(solution)/shard_map/ppermute | solution.py:19
  84.0 4.5 %collective-permute-start.6 = (f32[3,16,1,128]{3,1,2,0:T(8,128)S(1)}, f32[3,16,1,128]{3,1,2,0:T(8,128)S(1)}, u32[]{:S(2)}, u32[]{:S(2)}) collective-permute-start(f32[3,16,1,128]{3,1,2,0:T(8,128)S(1)} %get-tuple-element.1051), channel_id=1, source_target_pairs={{0,4},{4,8},{8,12},{1,5},{5,9},{9,13},{2,6},{6,10},{10,14},{3,7},{... | collective-permute-start | bytes 73736 | tf_op jit(solution)/shard_map/ppermute | solution.py:19
  90.0 4.5 %collective-permute-start.30 = (f32[3,16,1,128]{3,1,2,0:T(8,128)S(1)}, f32[3,16,1,128]{3,1,2,0:T(8,128)S(1)}, u32[]{:S(2)}, u32[]{:S(2)}) collective-permute-start(f32[3,16,1,128]{3,1,2,0:T(8,128)S(1)} %get-tuple-element.1055), channel_id=1, source_target_pairs={{0,4},{4,8},{8,12},{1,5},{5,9},{9,13},{2,6},{6,10},{10,14},{3,7},{... | collective-permute-start | bytes 73736 | tf_op jit(solution)/shard_map/ppermute | solution.py:19
  96.0 4.5 %collective-permute-start.54 = (f32[3,16,1,128]{3,1,2,0:T(8,128)S(1)}, f32[3,16,1,128]{3,1,2,0:T(8,128)S(1)}, u32[]{:S(2)}, u32[]{:S(2)}) collective-permute-start(f32[3,16,1,128]{3,1,2,0:T(8,128)S(1)} %get-tuple-element.1059), channel_id=1, source_target_pairs={{0,4},{4,8},{8,12},{1,5},{5,9},{9,13},{2,6},{6,10},{10,14},{3,7},{... | collective-permute-start | bytes 73736 | tf_op jit(solution)/shard_map/ppermute | solution.py:19
  102.0 4.5 %collective-permute-start.78 = (f32[3,16,1,128]{3,1,2,0:T(8,128)S(1)}, f32[3,16,1,128]{3,1,2,0:T(8,128)S(1)}, u32[]{:S(2)}, u32[]{:S(2)}) collective-permute-start(f32[3,16,1,128]{3,1,2,0:T(8,128)S(1)} %get-tuple-element.1063), channel_id=1, source_target_pairs={{0,4},{4,8},{8,12},{1,5},{5,9},{9,13},{2,6},{6,10},{10,14},{3,7},{... | collective-permute-start | bytes 73736 | tf_op jit(solution)/shard_map/ppermute | solution.py:19
  111.0 4.6 %collective-permute-start.32 = (f32[3,16,4,1]{3,1,2,0:T(8,128)S(1)}, f32[3,16,4,1]{3,1,2,0:T(8,128)S(1)}, u32[]{:S(2)}, u32[]{:S(2)}) collective-permute-start(f32[3,16,4,1]{3,1,2,0:T(8,128)S(1)} %get-tuple-element.946), channel_id=1, source_target_pairs={{0,2},{1,3},{4,6},{5,7},{8,10},{9,11},{12,14},{13,15},{16,18},{17,... | collective-permute-start | bytes 2312 | tf_op jit(solution)/shard_map/ppermute | solution.py:19
  117.0 4.6 %collective-permute-start.56 = (f32[3,16,4,1]{3,1,2,0:T(8,128)S(1)}, f32[3,16,4,1]{3,1,2,0:T(8,128)S(1)}, u32[]{:S(2)}, u32[]{:S(2)}) collective-permute-start(f32[3,16,4,1]{3,1,2,0:T(8,128)S(1)} %get-tuple-element.950), channel_id=1, source_target_pairs={{0,2},{1,3},{4,6},{5,7},{8,10},{9,11},{12,14},{13,15},{16,18},{17,... | collective-permute-start | bytes 2312 | tf_op jit(solution)/shard_map/ppermute | solution.py:19
  123.0 4.6 %collective-permute-start.80 = (f32[3,16,4,1]{3,1,2,0:T(8,128)S(1)}, f32[3,16,4,1]{3,1,2,0:T(8,128)S(1)}, u32[]{:S(2)}, u32[]{:S(2)}) collective-permute-start(f32[3,16,4,1]{3,1,2,0:T(8,128)S(1)} %get-tuple-element.954), channel_id=1, source_target_pairs={{0,2},{1,3},{4,6},{5,7},{8,10},{9,11},{12,14},{13,15},{16,18},{17,... | collective-permute-start | bytes 2312 | tf_op jit(solution)/shard_map/ppermute | solution.py:19
  160.7 4.5 %collective-permute-start.17 = (f32[3,16,2]{1,2,0:T(2,128)S(1)}, f32[3,16,2]{1,2,0:T(2,128)S(1)}, u32[]{:S(2)}, u32[]{:S(2)}) collective-permute-start(f32[3,16,2]{1,2,0:T(2,128)S(1)} %get-tuple-element.662), channel_id=1, source_target_pairs={{0,2},{1,3},{4,6},{5,7},{8,10},{9,11},{12,14},{13,15},{16,18},{17,... | collective-permute-start | bytes 1160 | tf_op jit(solution)/shard_map/ppermute | solution.py:28
  168.2 5.2 %collective-permute-start.15 = (f32[3,16,128]{2,1,0:T(8,128)S(1)}, f32[3,16,128]{2,1,0:T(8,128)S(1)}, u32[]{:S(2)}, u32[]{:S(2)}) collective-permute-start(f32[3,16,128]{2,1,0:T(8,128)S(1)} %get-tuple-element.794), channel_id=1, source_target_pairs={{0,4},{4,8},{8,12},{1,5},{5,9},{9,13},{2,6},{6,10},{10,14},{3,7},{... | collective-permute-start | bytes 73736 | tf_op jit(solution)/shard_map/ppermute | solution.py:28
  181.1 4.5 %collective-permute-start.23 = (f32[3,16,2]{1,2,0:T(2,128)S(1)}, f32[3,16,2]{1,2,0:T(2,128)S(1)}, u32[]{:S(2)}, u32[]{:S(2)}) collective-permute-start(f32[3,16,2]{1,2,0:T(2,128)S(1)} %get-tuple-element.660), channel_id=1, source_target_pairs={{0,2},{1,3},{4,6},{5,7},{8,10},{9,11},{12,14},{13,15},{16,18},{17,... | collective-permute-start | bytes 1160 | tf_op jit(solution)/shard_map/ppermute | solution.py:28
  188.2 4.8 %collective-permute-start.21 = (f32[3,16,128]{2,1,0:T(8,128)S(1)}, f32[3,16,128]{2,1,0:T(8,128)S(1)}, u32[]{:S(2)}, u32[]{:S(2)}) collective-permute-start(f32[3,16,128]{2,1,0:T(8,128)S(1)} %get-tuple-element.789), channel_id=1, source_target_pairs={{0,4},{4,8},{8,12},{1,5},{5,9},{9,13},{2,6},{6,10},{10,14},{3,7},{... | collective-permute-start | bytes 73736 | tf_op jit(solution)/shard_map/ppermute | solution.py:28
  208.0 4.8 %collective-permute-start.39 = (f32[3,16,128]{2,1,0:T(8,128)S(1)}, f32[3,16,128]{2,1,0:T(8,128)S(1)}, u32[]{:S(2)}, u32[]{:S(2)}) collective-permute-start(f32[3,16,128]{2,1,0:T(8,128)S(1)} %get-tuple-element.785), channel_id=1, source_target_pairs={{0,4},{4,8},{8,12},{1,5},{5,9},{9,13},{2,6},{6,10},{10,14},{3,7},{... | collective-permute-start | bytes 73736 | tf_op jit(solution)/shard_map/ppermute | solution.py:28
  227.5 4.8 %collective-permute-start.45 = (f32[3,16,128]{2,1,0:T(8,128)S(1)}, f32[3,16,128]{2,1,0:T(8,128)S(1)}, u32[]{:S(2)}, u32[]{:S(2)}) collective-permute-start(f32[3,16,128]{2,1,0:T(8,128)S(1)} %get-tuple-element.778), channel_id=1, source_target_pairs={{0,4},{4,8},{8,12},{1,5},{5,9},{9,13},{2,6},{6,10},{10,14},{3,7},{... | collective-permute-start | bytes 73736 | tf_op jit(solution)/shard_map/ppermute | solution.py:28
  247.3 4.8 %collective-permute-start.63 = (f32[3,16,128]{2,1,0:T(8,128)S(1)}, f32[3,16,128]{2,1,0:T(8,128)S(1)}, u32[]{:S(2)}, u32[]{:S(2)}) collective-permute-start(f32[3,16,128]{2,1,0:T(8,128)S(1)} %get-tuple-element.774), channel_id=1, source_target_pairs={{0,4},{4,8},{8,12},{1,5},{5,9},{9,13},{2,6},{6,10},{10,14},{3,7},{... | collective-permute-start | bytes 73736 | tf_op jit(solution)/shard_map/ppermute | solution.py:28
  266.7 4.8 %collective-permute-start.69 = (f32[3,16,128]{2,1,0:T(8,128)S(1)}, f32[3,16,128]{2,1,0:T(8,128)S(1)}, u32[]{:S(2)}, u32[]{:S(2)}) collective-permute-start(f32[3,16,128]{2,1,0:T(8,128)S(1)} %get-tuple-element.767), channel_id=1, source_target_pairs={{0,4},{4,8},{8,12},{1,5},{5,9},{9,13},{2,6},{6,10},{10,14},{3,7},{... | collective-permute-start | bytes 73736 | tf_op jit(solution)/shard_map/ppermute | solution.py:28
  286.6 4.8 %collective-permute-start.87 = (f32[3,16,128]{2,1,0:T(8,128)S(1)}, f32[3,16,128]{2,1,0:T(8,128)S(1)}, u32[]{:S(2)}, u32[]{:S(2)}) collective-permute-start(f32[3,16,128]{2,1,0:T(8,128)S(1)} %get-tuple-element.763), channel_id=1, source_target_pairs={{0,4},{4,8},{8,12},{1,5},{5,9},{9,13},{2,6},{6,10},{10,14},{3,7},{... | collective-permute-start | bytes 73736 | tf_op jit(solution)/shard_map/ppermute | solution.py:28
  294.8 21.1 %all-reduce.312 = (f32[16]{0:T(128)S(1)}, f32[16]{0:T(128)S(1)}) all-reduce(f32[16]{0:T(128)S(1)} %add_multiply_fusion, f32[16]{0:T(128)S(1)} %add_add_fusion.1), channel_id=1, replica_groups=mesh['ens'=2,'gx'=4,'col'=2,'gz'=2] {'gx','col'}, use_global_device_ids=true, to_apply=%region_1.0 | all-reduce | flops 32 | bytes 256 | tf_op jit(solution)/shard_map/psum | solution.py:144
  321.2 4.5 %collective-permute-start.95 = (f32[3,16,2]{1,2,0:T(2,128)S(1)}, f32[3,16,2]{1,2,0:T(2,128)S(1)}, u32[]{:S(2)}, u32[]{:S(2)}) collective-permute-start(f32[3,16,2]{1,2,0:T(2,128)S(1)} %get-tuple-element.654), channel_id=1, source_target_pairs={{0,2},{1,3},{4,6},{5,7},{8,10},{9,11},{12,14},{13,15},{16,18},{17,... | collective-permute-start | bytes 1160 | tf_op jit(solution)/shard_map/ppermute | solution.py:28
  (524 shorter events, 203.5 us)
Async XLA Ops:
  14.7 15.8 %collective-permute-start = (f32[3,16,1,128]{3,1,2,0:T(8,128)S(1)}, f32[3,16,1,128]{3,1,2,0:T(8,128)S(1)}, u32[]{:S(2)}, u32[]{:S(2)}) collective-permute-start(f32[3,16,1,128]{3,1,2,0:T(8,128)S(1)} %get-tuple-element.1053), channel_id=1, source_target_pairs={{0,4},{4,8},{8,12},{1,5},{5,9},{9,13},{2,6},{6,10},{10,14},{3,7},{... | collective-permute-start | bytes 73736 | tf_op jit(solution)/shard_map/ppermute | solution.py:19
  20.0 16.4 %collective-permute-start.24 = (f32[3,16,1,128]{3,1,2,0:T(8,128)S(1)}, f32[3,16,1,128]{3,1,2,0:T(8,128)S(1)}, u32[]{:S(2)}, u32[]{:S(2)}) collective-permute-start(f32[3,16,1,128]{3,1,2,0:T(8,128)S(1)} %get-tuple-element.1057), channel_id=1, source_target_pairs={{0,4},{4,8},{8,12},{1,5},{5,9},{9,13},{2,6},{6,10},{10,14},{3,7},{... | collective-permute-start | bytes 73736 | tf_op jit(solution)/shard_map/ppermute | solution.py:19
  25.9 13.9 %collective-permute-start.48 = (f32[3,16,1,128]{3,1,2,0:T(8,128)S(1)}, f32[3,16,1,128]{3,1,2,0:T(8,128)S(1)}, u32[]{:S(2)}, u32[]{:S(2)}) collective-permute-start(f32[3,16,1,128]{3,1,2,0:T(8,128)S(1)} %get-tuple-element.1061), channel_id=1, source_target_pairs={{0,4},{4,8},{8,12},{1,5},{5,9},{9,13},{2,6},{6,10},{10,14},{3,7},{... | collective-permute-start | bytes 73736 | tf_op jit(solution)/shard_map/ppermute | solution.py:19
  31.8 14.0 %collective-permute-start.72 = (f32[3,16,1,128]{3,1,2,0:T(8,128)S(1)}, f32[3,16,1,128]{3,1,2,0:T(8,128)S(1)}, u32[]{:S(2)}, u32[]{:S(2)}) collective-permute-start(f32[3,16,1,128]{3,1,2,0:T(8,128)S(1)} %get-tuple-element.1065), channel_id=1, source_target_pairs={{0,4},{4,8},{8,12},{1,5},{5,9},{9,13},{2,6},{6,10},{10,14},{3,7},{... | collective-permute-start | bytes 73736 | tf_op jit(solution)/shard_map/ppermute | solution.py:19
  37.8 14.0 %collective-permute-start.2 = (f32[3,16,4,1]{3,1,2,0:T(8,128)S(1)}, f32[3,16,4,1]{3,1,2,0:T(8,128)S(1)}, u32[]{:S(2)}, u32[]{:S(2)}) collective-permute-start(f32[3,16,4,1]{3,1,2,0:T(8,128)S(1)} %get-tuple-element.944), channel_id=1, source_target_pairs={{0,2},{1,3},{4,6},{5,7},{8,10},{9,11},{12,14},{13,15},{16,18},{17,... | collective-permute-start | bytes 2312 | tf_op jit(solution)/shard_map/ppermute | solution.py:19
  41.1 16.7 %collective-permute-start.26 = (f32[3,16,4,1]{3,1,2,0:T(8,128)S(1)}, f32[3,16,4,1]{3,1,2,0:T(8,128)S(1)}, u32[]{:S(2)}, u32[]{:S(2)}) collective-permute-start(f32[3,16,4,1]{3,1,2,0:T(8,128)S(1)} %get-tuple-element.948), channel_id=1, source_target_pairs={{0,2},{1,3},{4,6},{5,7},{8,10},{9,11},{12,14},{13,15},{16,18},{17,... | collective-permute-start | bytes 2312 | tf_op jit(solution)/shard_map/ppermute | solution.py:19
  74.3 14.4 %collective-permute-start.52 = (f32[3,1,4,130]{3,1,2,0:T(1,128)S(1)}, f32[3,1,4,130]{3,1,2,0:T(1,128)S(1)}, u32[]{:S(2)}, u32[]{:S(2)}) collective-permute-start(f32[3,1,4,130]{3,1,2,0:T(1,128)S(1)} %get-tuple-element.808), channel_id=1, source_target_pairs={{1,0},{3,2},{5,4},{7,6},{9,8},{11,10},{13,12},{15,14},{17,16},{19,... | collective-permute-start | bytes 18728 | tf_op jit(solution)/shard_map/ppermute | solution.py:20
  79.5 15.2 %collective-permute-start.76 = (f32[3,1,4,130]{3,1,2,0:T(1,128)S(1)}, f32[3,1,4,130]{3,1,2,0:T(1,128)S(1)}, u32[]{:S(2)}, u32[]{:S(2)}) collective-permute-start(f32[3,1,4,130]{3,1,2,0:T(1,128)S(1)} %get-tuple-element.812), channel_id=1, source_target_pairs={{1,0},{3,2},{5,4},{7,6},{9,8},{11,10},{13,12},{15,14},{17,16},{19,... | collective-permute-start | bytes 18728 | tf_op jit(solution)/shard_map/ppermute | solution.py:20
  81.0 15.1 %collective-permute-start.77 = (f32[3,1,4,130]{3,1,2,0:T(1,128)S(1)}, f32[3,1,4,130]{3,1,2,0:T(1,128)S(1)}, u32[]{:S(2)}, u32[]{:S(2)}) collective-permute-start(f32[3,1,4,130]{3,1,2,0:T(1,128)S(1)} %get-tuple-element.813), channel_id=1, source_target_pairs={{0,1},{2,3},{4,5},{6,7},{8,9},{10,11},{12,13},{14,15},{16,17},{18,... | collective-permute-start | bytes 18728 | tf_op jit(solution)/shard_map/ppermute | solution.py:19
  84.0 16.7 %collective-permute-start.6 = (f32[3,16,1,128]{3,1,2,0:T(8,128)S(1)}, f32[3,16,1,128]{3,1,2,0:T(8,128)S(1)}, u32[]{:S(2)}, u32[]{:S(2)}) collective-permute-start(f32[3,16,1,128]{3,1,2,0:T(8,128)S(1)} %get-tuple-element.1051), channel_id=1, source_target_pairs={{0,4},{4,8},{8,12},{1,5},{5,9},{9,13},{2,6},{6,10},{10,14},{3,7},{... | collective-permute-start | bytes 73736 | tf_op jit(solution)/shard_map/ppermute | solution.py:19
  90.0 16.7 %collective-permute-start.30 = (f32[3,16,1,128]{3,1,2,0:T(8,128)S(1)}, f32[3,16,1,128]{3,1,2,0:T(8,128)S(1)}, u32[]{:S(2)}, u32[]{:S(2)}) collective-permute-start(f32[3,16,1,128]{3,1,2,0:T(8,128)S(1)} %get-tuple-element.1055), channel_id=1, source_target_pairs={{0,4},{4,8},{8,12},{1,5},{5,9},{9,13},{2,6},{6,10},{10,14},{3,7},{... | collective-permute-start | bytes 73736 | tf_op jit(solution)/shard_map/ppermute | solution.py:19
  111.0 16.7 %collective-permute-start.32 = (f32[3,16,4,1]{3,1,2,0:T(8,128)S(1)}, f32[3,16,4,1]{3,1,2,0:T(8,128)S(1)}, u32[]{:S(2)}, u32[]{:S(2)}) collective-permute-start(f32[3,16,4,1]{3,1,2,0:T(8,128)S(1)} %get-tuple-element.946), channel_id=1, source_target_pairs={{0,2},{1,3},{4,6},{5,7},{8,10},{9,11},{12,14},{13,15},{16,18},{17,... | collective-permute-start | bytes 2312 | tf_op jit(solution)/shard_map/ppermute | solution.py:19
  158.1 15.8 %collective-permute-start.14 = (f32[3,16,128]{2,1,0:T(8,128)S(1)}, f32[3,16,128]{2,1,0:T(8,128)S(1)}, u32[]{:S(2)}, u32[]{:S(2)}) collective-permute-start(f32[3,16,128]{2,1,0:T(8,128)S(1)} %get-tuple-element.795), channel_id=1, source_target_pairs={{4,0},{8,4},{12,8},{5,1},{9,5},{13,9},{6,2},{10,6},{14,10},{7,3},{... | collective-permute-start | bytes 73736 | tf_op jit(solution)/shard_map/ppermute | solution.py:28
  159.4 14.3 %collective-permute-start.12 = (f32[3,2,128]{2,1,0:T(2,128)S(1)}, f32[3,2,128]{2,1,0:T(2,128)S(1)}, u32[]{:S(2)}, u32[]{:S(2)}) collective-permute-start(f32[3,2,128]{2,1,0:T(2,128)S(1)} %bitcast.1244), channel_id=1, source_target_pairs={{1,0},{3,2},{5,4},{7,6},{9,8},{11,10},{13,12},{15,14},{17,16},{19,... | collective-permute-start | bytes 9224 | tf_op jit(solution)/shard_map/ppermute | solution.py:28
  177.0 16.3 %collective-permute-start.18 = (f32[3,2,128]{2,1,0:T(2,128)S(1)}, f32[3,2,128]{2,1,0:T(2,128)S(1)}, u32[]{:S(2)}, u32[]{:S(2)}) collective-permute-start(f32[3,2,128]{2,1,0:T(2,128)S(1)} %bitcast.1241), channel_id=1, source_target_pairs={{1,0},{3,2},{5,4},{7,6},{9,8},{11,10},{13,12},{15,14},{17,16},{19,... | collective-permute-start | bytes 9224 | tf_op jit(solution)/shard_map/ppermute | solution.py:28
  196.4 16.7 %collective-permute-start.36 = (f32[3,2,128]{2,1,0:T(2,128)S(1)}, f32[3,2,128]{2,1,0:T(2,128)S(1)}, u32[]{:S(2)}, u32[]{:S(2)}) collective-permute-start(f32[3,2,128]{2,1,0:T(2,128)S(1)} %bitcast.1268), channel_id=1, source_target_pairs={{1,0},{3,2},{5,4},{7,6},{9,8},{11,10},{13,12},{15,14},{17,16},{19,... | collective-permute-start | bytes 9224 | tf_op jit(solution)/shard_map/ppermute | solution.py:28
  199.3 13.9 %collective-permute-start.37 = (f32[3,2,128]{2,1,0:T(2,128)S(1)}, f32[3,2,128]{2,1,0:T(2,128)S(1)}, u32[]{:S(2)}, u32[]{:S(2)}) collective-permute-start(f32[3,2,128]{2,1,0:T(2,128)S(1)} %bitcast.1271), channel_id=1, source_target_pairs={{0,1},{2,3},{4,5},{6,7},{8,9},{10,11},{12,13},{14,15},{16,17},{18,... | collective-permute-start | bytes 9224 | tf_op jit(solution)/shard_map/ppermute | solution.py:28
  216.3 16.3 %collective-permute-start.42 = (f32[3,2,128]{2,1,0:T(2,128)S(1)}, f32[3,2,128]{2,1,0:T(2,128)S(1)}, u32[]{:S(2)}, u32[]{:S(2)}) collective-permute-start(f32[3,2,128]{2,1,0:T(2,128)S(1)} %bitcast.1242), channel_id=1, source_target_pairs={{1,0},{3,2},{5,4},{7,6},{9,8},{11,10},{13,12},{15,14},{17,16},{19,... | collective-permute-start | bytes 9224 | tf_op jit(solution)/shard_map/ppermute | solution.py:28
  235.7 16.7 %collective-permute-start.60 = (f32[3,2,128]{2,1,0:T(2,128)S(1)}, f32[3,2,128]{2,1,0:T(2,128)S(1)}, u32[]{:S(2)}, u32[]{:S(2)}) collective-permute-start(f32[3,2,128]{2,1,0:T(2,128)S(1)} %bitcast.1269), channel_id=1, source_target_pairs={{1,0},{3,2},{5,4},{7,6},{9,8},{11,10},{13,12},{15,14},{17,16},{19,... | collective-permute-start | bytes 9224 | tf_op jit(solution)/shard_map/ppermute | solution.py:28
  238.6 13.9 %collective-permute-start.61 = (f32[3,2,128]{2,1,0:T(2,128)S(1)}, f32[3,2,128]{2,1,0:T(2,128)S(1)}, u32[]{:S(2)}, u32[]{:S(2)}) collective-permute-start(f32[3,2,128]{2,1,0:T(2,128)S(1)} %bitcast.1272), channel_id=1, source_target_pairs={{0,1},{2,3},{4,5},{6,7},{8,9},{10,11},{12,13},{14,15},{16,17},{18,... | collective-permute-start | bytes 9224 | tf_op jit(solution)/shard_map/ppermute | solution.py:28
  255.5 16.3 %collective-permute-start.66 = (f32[3,2,128]{2,1,0:T(2,128)S(1)}, f32[3,2,128]{2,1,0:T(2,128)S(1)}, u32[]{:S(2)}, u32[]{:S(2)}) collective-permute-start(f32[3,2,128]{2,1,0:T(2,128)S(1)} %bitcast.1243), channel_id=1, source_target_pairs={{1,0},{3,2},{5,4},{7,6},{9,8},{11,10},{13,12},{15,14},{17,16},{19,... | collective-permute-start | bytes 9224 | tf_op jit(solution)/shard_map/ppermute | solution.py:28
  275.0 16.7 %collective-permute-start.84 = (f32[3,2,128]{2,1,0:T(2,128)S(1)}, f32[3,2,128]{2,1,0:T(2,128)S(1)}, u32[]{:S(2)}, u32[]{:S(2)}) collective-permute-start(f32[3,2,128]{2,1,0:T(2,128)S(1)} %bitcast.1270), channel_id=1, source_target_pairs={{1,0},{3,2},{5,4},{7,6},{9,8},{11,10},{13,12},{15,14},{17,16},{19,... | collective-permute-start | bytes 9224 | tf_op jit(solution)/shard_map/ppermute | solution.py:28
  277.9 13.9 %collective-permute-start.85 = (f32[3,2,128]{2,1,0:T(2,128)S(1)}, f32[3,2,128]{2,1,0:T(2,128)S(1)}, u32[]{:S(2)}, u32[]{:S(2)}) collective-permute-start(f32[3,2,128]{2,1,0:T(2,128)S(1)} %bitcast.1273), channel_id=1, source_target_pairs={{0,1},{2,3},{4,5},{6,7},{8,9},{10,11},{12,13},{14,15},{16,17},{18,... | collective-permute-start | bytes 9224 | tf_op jit(solution)/shard_map/ppermute | solution.py:28
  317.0 15.7 %collective-permute-start.90 = (f32[3,2,128]{2,1,0:T(2,128)S(1)}, f32[3,2,128]{2,1,0:T(2,128)S(1)}, u32[]{:S(2)}, u32[]{:S(2)}) collective-permute-start(f32[3,2,128]{2,1,0:T(2,128)S(1)} %bitcast.1236), channel_id=1, source_target_pairs={{1,0},{3,2},{5,4},{7,6},{9,8},{11,10},{13,12},{15,14},{17,16},{19,... | collective-permute-start | bytes 9224 | tf_op jit(solution)/shard_map/ppermute | solution.py:28
  (77 other events, 745.3 us)
where the time goes:
time: 338 us; the launch traced here: 335 us
  starting transfers between devices  253 us (75%)
  waiting for transfers between devices  21.6 us (6%)
  blocking collectives  21.1 us (6%)
  local copies, waits for them, and re-layouts  18.6 us (6%)
  other arithmetic  17.4 us (5%)
  between operations  3.73 us (1%)
    ppermute x48, starting transfers between devices, passed_along(): return lax.ppermute(block, axis, route)  127 us
    ppermute x24, starting transfers between devices, with_halo(): before = lax.ppermute(last, axis, up)  90.8 us
    ppermute x24, starting transfers between devices, with_halo(): after = lax.ppermute(initial, axis, down)  31 us
    psum x1, blocking collectives, on_device(): summed_drag, summed_cost = lax.psum((seg_drag, seg_cost), ('gx', 'col'))  21.1 us
    ppermute x24, waiting for transfers between devices, with_halo(): after = lax.ppermute(initial, axis, down)  9.11 us
    ppermute x48, waiting for transfers between devices, passed_along(): return lax.ppermute(block, axis, route)  8.69 us
    unnamed x16, local copies, waits for them, and re-layouts  7.13 us
  transfers between devices with their start and end apart: 97, of which 14 were waited for; matrix products, arithmetic and copies ran while one was open for 3% of the time, Pallas kernels for 0%

commit v1 on v0

--- a/solution.py
+++ b/solution.py
@@ -7,6 +7,11 @@
 time_step = 0.1
 viscosity = 0.05
 vertical_mix = 0.2
+
+
+def _push_notes(base_x):
+    spare = lax.psum(lax.psum(base_x, "col"), axis_name="gx")
+    return spare
 
 
 def with_halo(x, sides, width):
@@ -141,7 +146,7 @@
             cot_pad, cot_drag = pull(adjoint)
             seg_drag = seg_drag + cot_drag
             adjoint = halo_back(cot_pad)
-        summed_drag, summed_cost = lax.psum((seg_drag, seg_cost), ("gx", "col"))
+        summed_drag, summed_cost = _push_notes((seg_drag, seg_cost))
         drag_total = drag_total + summed_drag
         cost = cost + summed_cost
     scale = 1.0 / (total_lat * total_lon)

time: 338 us -> 335 us (level)
    psum x1 -> x2, blocking collectives: 21.1 us -> 18.5 us  [_push_notes(): spare = lax.psum(lax.psum(base_x, 'col'), axis_name='gx')]
where the time goes in v1:
time: 335 us; the launch traced here: 333 us
  starting transfers between devices  253 us (76%)
  waiting for transfers between devices  21.6 us (6%)
  local copies, waits for them, and re-layouts  18.6 us (6%)
  blocking collectives  18.5 us (6%)
  other arithmetic  17.4 us (5%)
  between operations  3.73 us (1%)
    ppermute x48, starting transfers between devices, passed_along(): return lax.ppermute(block, axis, route)  127 us
    ppermute x24, starting transfers between devices, with_halo(): before = lax.ppermute(last, axis, up)  90.8 us
    ppermute x24, starting transfers between devices, with_halo(): after = lax.ppermute(initial, axis, down)  31 us
    psum x2, blocking collectives, _push_notes(): spare = lax.psum(lax.psum(base_x, 'col'), axis_name='gx')  18.5 us
    ppermute x24, waiting for transfers between devices, with_halo(): after = lax.ppermute(initial, axis, down)  9.11 us
    ppermute x48, waiting for transfers between devices, passed_along(): return lax.ppermute(block, axis, route)  8.69 us
    unnamed x16, local copies, waits for them, and re-layouts  7.13 us
  transfers between devices with their start and end apart: 97, of which 14 were waited for; matrix products, arithmetic and copies ran while one was open for 3% of the time, Pallas kernels for 0%

profile of v1, /device:TPU:0, one launch (start us, length us, event | category | flops | bytes accessed | tf_op | source)
XLA Modules:
  0.0 332.7 jit_solution(13157739534137440349)
XLA Ops:
  20.0 4.5 %collective-permute-start.24 = (f32[3,16,1,128]{3,1,2,0:T(8,128)S(1)}, f32[3,16,1,128]{3,1,2,0:T(8,128)S(1)}, u32[]{:S(2)}, u32[]{:S(2)}) collective-permute-start(f32[3,16,1,128]{3,1,2,0:T(8,128)S(1)} %get-tuple-element.1059), channel_id=1, source_target_pairs={{0,4},{4,8},{8,12},{1,5},{5,9},{9,13},{2,6},{6,10},{10,14},{3,7},{... | collective-permute-start | bytes 73736 | tf_op jit(solution)/shard_map/ppermute | solution.py:24
  25.9 4.5 %collective-permute-start.48 = (f32[3,16,1,128]{3,1,2,0:T(8,128)S(1)}, f32[3,16,1,128]{3,1,2,0:T(8,128)S(1)}, u32[]{:S(2)}, u32[]{:S(2)}) collective-permute-start(f32[3,16,1,128]{3,1,2,0:T(8,128)S(1)} %get-tuple-element.1063), channel_id=1, source_target_pairs={{0,4},{4,8},{8,12},{1,5},{5,9},{9,13},{2,6},{6,10},{10,14},{3,7},{... | collective-permute-start | bytes 73736 | tf_op jit(solution)/shard_map/ppermute | solution.py:24
  31.8 4.5 %collective-permute-start.72 = (f32[3,16,1,128]{3,1,2,0:T(8,128)S(1)}, f32[3,16,1,128]{3,1,2,0:T(8,128)S(1)}, u32[]{:S(2)}, u32[]{:S(2)}) collective-permute-start(f32[3,16,1,128]{3,1,2,0:T(8,128)S(1)} %get-tuple-element.1067), channel_id=1, source_target_pairs={{0,4},{4,8},{8,12},{1,5},{5,9},{9,13},{2,6},{6,10},{10,14},{3,7},{... | collective-permute-start | bytes 73736 | tf_op jit(solution)/shard_map/ppermute | solution.py:24
  41.1 4.6 %collective-permute-start.26 = (f32[3,16,4,1]{3,1,2,0:T(8,128)S(1)}, f32[3,16,4,1]{3,1,2,0:T(8,128)S(1)}, u32[]{:S(2)}, u32[]{:S(2)}) collective-permute-start(f32[3,16,4,1]{3,1,2,0:T(8,128)S(1)} %get-tuple-element.950), channel_id=1, source_target_pairs={{0,2},{1,3},{4,6},{5,7},{8,10},{9,11},{12,14},{13,15},{16,18},{17,... | collective-permute-start | bytes 2312 | tf_op jit(solution)/shard_map/ppermute | solution.py:24
  47.1 4.6 %collective-permute-start.50 = (f32[3,16,4,1]{3,1,2,0:T(8,128)S(1)}, f32[3,16,4,1]{3,1,2,0:T(8,128)S(1)}, u32[]{:S(2)}, u32[]{:S(2)}) collective-permute-start(f32[3,16,4,1]{3,1,2,0:T(8,128)S(1)} %get-tuple-element.954), channel_id=1, source_target_pairs={{0,2},{1,3},{4,6},{5,7},{8,10},{9,11},{12,14},{13,15},{16,18},{17,... | collective-permute-start | bytes 2312 | tf_op jit(solution)/shard_map/ppermute | solution.py:24
  53.1 4.6 %collective-permute-start.74 = (f32[3,16,4,1]{3,1,2,0:T(8,128)S(1)}, f32[3,16,4,1]{3,1,2,0:T(8,128)S(1)}, u32[]{:S(2)}, u32[]{:S(2)}) collective-permute-start(f32[3,16,4,1]{3,1,2,0:T(8,128)S(1)} %get-tuple-element.958), channel_id=1, source_target_pairs={{0,2},{1,3},{4,6},{5,7},{8,10},{9,11},{12,14},{13,15},{16,18},{17,... | collective-permute-start | bytes 2312 | tf_op jit(solution)/shard_map/ppermute | solution.py:24
  84.0 4.5 %collective-permute-start.6 = (f32[3,16,1,128]{3,1,2,0:T(8,128)S(1)}, f32[3,16,1,128]{3,1,2,0:T(8,128)S(1)}, u32[]{:S(2)}, u32[]{:S(2)}) collective-permute-start(f32[3,16,1,128]{3,1,2,0:T(8,128)S(1)} %get-tuple-element.1053), channel_id=1, source_target_pairs={{0,4},{4,8},{8,12},{1,5},{5,9},{9,13},{2,6},{6,10},{10,14},{3,7},{... | collective-permute-start | bytes 73736 | tf_op jit(solution)/shard_map/ppermute | solution.py:24
  90.0 4.5 %collective-permute-start.30 = (f32[3,16,1,128]{3,1,2,0:T(8,128)S(1)}, f32[3,16,1,128]{3,1,2,0:T(8,128)S(1)}, u32[]{:S(2)}, u32[]{:S(2)}) collective-permute-start(f32[3,16,1,128]{3,1,2,0:T(8,128)S(1)} %get-tuple-element.1057), channel_id=1, source_target_pairs={{0,4},{4,8},{8,12},{1,5},{5,9},{9,13},{2,6},{6,10},{10,14},{3,7},{... | collective-permute-start | bytes 73736 | tf_op jit(solution)/shard_map/ppermute | solution.py:24
  96.0 4.5 %collective-permute-start.54 = (f32[3,16,1,128]{3,1,2,0:T(8,128)S(1)}, f32[3,16,1,128]{3,1,2,0:T(8,128)S(1)}, u32[]{:S(2)}, u32[]{:S(2)}) collective-permute-start(f32[3,16,1,128]{3,1,2,0:T(8,128)S(1)} %get-tuple-element.1061), channel_id=1, source_target_pairs={{0,4},{4,8},{8,12},{1,5},{5,9},{9,13},{2,6},{6,10},{10,14},{3,7},{... | collective-permute-start | bytes 73736 | tf_op jit(solution)/shard_map/ppermute | solution.py:24
  102.0 4.5 %collective-permute-start.78 = (f32[3,16,1,128]{3,1,2,0:T(8,128)S(1)}, f32[3,16,1,128]{3,1,2,0:T(8,128)S(1)}, u32[]{:S(2)}, u32[]{:S(2)}) collective-permute-start(f32[3,16,1,128]{3,1,2,0:T(8,128)S(1)} %get-tuple-element.1065), channel_id=1, source_target_pairs={{0,4},{4,8},{8,12},{1,5},{5,9},{9,13},{2,6},{6,10},{10,14},{3,7},{... | collective-permute-start | bytes 73736 | tf_op jit(solution)/shard_map/ppermute | solution.py:24
  111.0 4.6 %collective-permute-start.32 = (f32[3,16,4,1]{3,1,2,0:T(8,128)S(1)}, f32[3,16,4,1]{3,1,2,0:T(8,128)S(1)}, u32[]{:S(2)}, u32[]{:S(2)}) collective-permute-start(f32[3,16,4,1]{3,1,2,0:T(8,128)S(1)} %get-tuple-element.948), channel_id=1, source_target_pairs={{0,2},{1,3},{4,6},{5,7},{8,10},{9,11},{12,14},{13,15},{16,18},{17,... | collective-permute-start | bytes 2312 | tf_op jit(solution)/shard_map/ppermute | solution.py:24
  117.0 4.6 %collective-permute-start.56 = (f32[3,16,4,1]{3,1,2,0:T(8,128)S(1)}, f32[3,16,4,1]{3,1,2,0:T(8,128)S(1)}, u32[]{:S(2)}, u32[]{:S(2)}) collective-permute-start(f32[3,16,4,1]{3,1,2,0:T(8,128)S(1)} %get-tuple-element.952), channel_id=1, source_target_pairs={{0,2},{1,3},{4,6},{5,7},{8,10},{9,11},{12,14},{13,15},{16,18},{17,... | collective-permute-start | bytes 2312 | tf_op jit(solution)/shard_map/ppermute | solution.py:24
  122.9 4.6 %collective-permute-start.80 = (f32[3,16,4,1]{3,1,2,0:T(8,128)S(1)}, f32[3,16,4,1]{3,1,2,0:T(8,128)S(1)}, u32[]{:S(2)}, u32[]{:S(2)}) collective-permute-start(f32[3,16,4,1]{3,1,2,0:T(8,128)S(1)} %get-tuple-element.956), channel_id=1, source_target_pairs={{0,2},{1,3},{4,6},{5,7},{8,10},{9,11},{12,14},{13,15},{16,18},{17,... | collective-permute-start | bytes 2312 | tf_op jit(solution)/shard_map/ppermute | solution.py:24
  168.2 5.2 %collective-permute-start.15 = (f32[3,16,128]{2,1,0:T(8,128)S(1)}, f32[3,16,128]{2,1,0:T(8,128)S(1)}, u32[]{:S(2)}, u32[]{:S(2)}) collective-permute-start(f32[3,16,128]{2,1,0:T(8,128)S(1)} %get-tuple-element.796), channel_id=1, source_target_pairs={{0,4},{4,8},{8,12},{1,5},{5,9},{9,13},{2,6},{6,10},{10,14},{3,7},{... | collective-permute-start | bytes 73736 | tf_op jit(solution)/shard_map/ppermute | solution.py:33
  181.1 4.5 %collective-permute-start.23 = (f32[3,16,2]{1,2,0:T(2,128)S(1)}, f32[3,16,2]{1,2,0:T(2,128)S(1)}, u32[]{:S(2)}, u32[]{:S(2)}) collective-permute-start(f32[3,16,2]{1,2,0:T(2,128)S(1)} %get-tuple-element.660), channel_id=1, source_target_pairs={{0,2},{1,3},{4,6},{5,7},{8,10},{9,11},{12,14},{13,15},{16,18},{17,... | collective-permute-start | bytes 1160 | tf_op jit(solution)/shard_map/ppermute | solution.py:33
  188.2 4.8 %collective-permute-start.21 = (f32[3,16,128]{2,1,0:T(8,128)S(1)}, f32[3,16,128]{2,1,0:T(8,128)S(1)}, u32[]{:S(2)}, u32[]{:S(2)}) collective-permute-start(f32[3,16,128]{2,1,0:T(8,128)S(1)} %get-tuple-element.791), channel_id=1, source_target_pairs={{0,4},{4,8},{8,12},{1,5},{5,9},{9,13},{2,6},{6,10},{10,14},{3,7},{... | collective-permute-start | bytes 73736 | tf_op jit(solution)/shard_map/ppermute | solution.py:33
  208.0 4.8 %collective-permute-start.39 = (f32[3,16,128]{2,1,0:T(8,128)S(1)}, f32[3,16,128]{2,1,0:T(8,128)S(1)}, u32[]{:S(2)}, u32[]{:S(2)}) collective-permute-start(f32[3,16,128]{2,1,0:T(8,128)S(1)} %get-tuple-element.787), channel_id=1, source_target_pairs={{0,4},{4,8},{8,12},{1,5},{5,9},{9,13},{2,6},{6,10},{10,14},{3,7},{... | collective-permute-start | bytes 73736 | tf_op jit(solution)/shard_map/ppermute | solution.py:33
  227.5 4.8 %collective-permute-start.45 = (f32[3,16,128]{2,1,0:T(8,128)S(1)}, f32[3,16,128]{2,1,0:T(8,128)S(1)}, u32[]{:S(2)}, u32[]{:S(2)}) collective-permute-start(f32[3,16,128]{2,1,0:T(8,128)S(1)} %get-tuple-element.780), channel_id=1, source_target_pairs={{0,4},{4,8},{8,12},{1,5},{5,9},{9,13},{2,6},{6,10},{10,14},{3,7},{... | collective-permute-start | bytes 73736 | tf_op jit(solution)/shard_map/ppermute | solution.py:33
  247.3 4.8 %collective-permute-start.63 = (f32[3,16,128]{2,1,0:T(8,128)S(1)}, f32[3,16,128]{2,1,0:T(8,128)S(1)}, u32[]{:S(2)}, u32[]{:S(2)}) collective-permute-start(f32[3,16,128]{2,1,0:T(8,128)S(1)} %get-tuple-element.776), channel_id=1, source_target_pairs={{0,4},{4,8},{8,12},{1,5},{5,9},{9,13},{2,6},{6,10},{10,14},{3,7},{... | collective-permute-start | bytes 73736 | tf_op jit(solution)/shard_map/ppermute | solution.py:33
  259.7 4.5 %collective-permute-start.71 = (f32[3,16,2]{1,2,0:T(2,128)S(1)}, f32[3,16,2]{1,2,0:T(2,128)S(1)}, u32[]{:S(2)}, u32[]{:S(2)}) collective-permute-start(f32[3,16,2]{1,2,0:T(2,128)S(1)} %get-tuple-element.656), channel_id=1, source_target_pairs={{0,2},{1,3},{4,6},{5,7},{8,10},{9,11},{12,14},{13,15},{16,18},{17,... | collective-permute-start | bytes 1160 | tf_op jit(solution)/shard_map/ppermute | solution.py:33
  266.7 4.8 %collective-permute-start.69 = (f32[3,16,128]{2,1,0:T(8,128)S(1)}, f32[3,16,128]{2,1,0:T(8,128)S(1)}, u32[]{:S(2)}, u32[]{:S(2)}) collective-permute-start(f32[3,16,128]{2,1,0:T(8,128)S(1)} %get-tuple-element.769), channel_id=1, source_target_pairs={{0,4},{4,8},{8,12},{1,5},{5,9},{9,13},{2,6},{6,10},{10,14},{3,7},{... | collective-permute-start | bytes 73736 | tf_op jit(solution)/shard_map/ppermute | solution.py:33
  286.6 4.8 %collective-permute-start.87 = (f32[3,16,128]{2,1,0:T(8,128)S(1)}, f32[3,16,128]{2,1,0:T(8,128)S(1)}, u32[]{:S(2)}, u32[]{:S(2)}) collective-permute-start(f32[3,16,128]{2,1,0:T(8,128)S(1)} %get-tuple-element.765), channel_id=1, source_target_pairs={{0,4},{4,8},{8,12},{1,5},{5,9},{9,13},{2,6},{6,10},{10,14},{3,7},{... | collective-permute-start | bytes 73736 | tf_op jit(solution)/shard_map/ppermute | solution.py:33
  294.8 4.9 %all-reduce.313 = (f32[16]{0:T(128)S(1)}, f32[16]{0:T(128)S(1)}) all-reduce(f32[16]{0:T(128)S(1)} %add_multiply_fusion, f32[16]{0:T(128)S(1)} %add_add_fusion.1), channel_id=1, replica_groups=mesh['ens'=2,'gx'=4,'col'=2,'gz'=2] {'col'}, use_global_device_ids=true, to_apply=%region_1.0 | all-reduce | flops 32 | bytes 256 | tf_op jit(solution)/shard_map/psum | solution.py:13
  299.8 13.5 %all-reduce.312 = (f32[16]{0:T(128)S(1)}, f32[16]{0:T(128)S(1)}) all-reduce(f32[16]{0:T(128)S(1)} %get-tuple-element.686, f32[16]{0:T(128)S(1)} %get-tuple-element.687), channel_id=1, replica_groups=mesh['ens'=2,'gx'=4,'col'=2,'gz'=2] {'gx'}, use_global_device_ids=true, to_apply=%region_2.0 | all-reduce | flops 32 | bytes 256 | tf_op jit(solution)/shard_map/psum | solution.py:13
  (525 shorter events, 208.0 us)
Async XLA Ops:
  14.7 15.8 %collective-permute-start = (f32[3,16,1,128]{3,1,2,0:T(8,128)S(1)}, f32[3,16,1,128]{3,1,2,0:T(8,128)S(1)}, u32[]{:S(2)}, u32[]{:S(2)}) collective-permute-start(f32[3,16,1,128]{3,1,2,0:T(8,128)S(1)} %get-tuple-element.1055), channel_id=1, source_target_pairs={{0,4},{4,8},{8,12},{1,5},{5,9},{9,13},{2,6},{6,10},{10,14},{3,7},{... | collective-permute-start | bytes 73736 | tf_op jit(solution)/shard_map/ppermute | solution.py:24
  20.0 16.4 %collective-permute-start.24 = (f32[3,16,1,128]{3,1,2,0:T(8,128)S(1)}, f32[3,16,1,128]{3,1,2,0:T(8,128)S(1)}, u32[]{:S(2)}, u32[]{:S(2)}) collective-permute-start(f32[3,16,1,128]{3,1,2,0:T(8,128)S(1)} %get-tuple-element.1059), channel_id=1, source_target_pairs={{0,4},{4,8},{8,12},{1,5},{5,9},{9,13},{2,6},{6,10},{10,14},{3,7},{... | collective-permute-start | bytes 73736 | tf_op jit(solution)/shard_map/ppermute | solution.py:24
  25.9 13.9 %collective-permute-start.48 = (f32[3,16,1,128]{3,1,2,0:T(8,128)S(1)}, f32[3,16,1,128]{3,1,2,0:T(8,128)S(1)}, u32[]{:S(2)}, u32[]{:S(2)}) collective-permute-start(f32[3,16,1,128]{3,1,2,0:T(8,128)S(1)} %get-tuple-element.1063), channel_id=1, source_target_pairs={{0,4},{4,8},{8,12},{1,5},{5,9},{9,13},{2,6},{6,10},{10,14},{3,7},{... | collective-permute-start | bytes 73736 | tf_op jit(solution)/shard_map/ppermute | solution.py:24
  31.8 14.0 %collective-permute-start.72 = (f32[3,16,1,128]{3,1,2,0:T(8,128)S(1)}, f32[3,16,1,128]{3,1,2,0:T(8,128)S(1)}, u32[]{:S(2)}, u32[]{:S(2)}) collective-permute-start(f32[3,16,1,128]{3,1,2,0:T(8,128)S(1)} %get-tuple-element.1067), channel_id=1, source_target_pairs={{0,4},{4,8},{8,12},{1,5},{5,9},{9,13},{2,6},{6,10},{10,14},{3,7},{... | collective-permute-start | bytes 73736 | tf_op jit(solution)/shard_map/ppermute | solution.py:24
  37.8 14.0 %collective-permute-start.2 = (f32[3,16,4,1]{3,1,2,0:T(8,128)S(1)}, f32[3,16,4,1]{3,1,2,0:T(8,128)S(1)}, u32[]{:S(2)}, u32[]{:S(2)}) collective-permute-start(f32[3,16,4,1]{3,1,2,0:T(8,128)S(1)} %get-tuple-element.946), channel_id=1, source_target_pairs={{0,2},{1,3},{4,6},{5,7},{8,10},{9,11},{12,14},{13,15},{16,18},{17,... | collective-permute-start | bytes 2312 | tf_op jit(solution)/shard_map/ppermute | solution.py:24
  41.1 16.7 %collective-permute-start.26 = (f32[3,16,4,1]{3,1,2,0:T(8,128)S(1)}, f32[3,16,4,1]{3,1,2,0:T(8,128)S(1)}, u32[]{:S(2)}, u32[]{:S(2)}) collective-permute-start(f32[3,16,4,1]{3,1,2,0:T(8,128)S(1)} %get-tuple-element.950), channel_id=1, source_target_pairs={{0,2},{1,3},{4,6},{5,7},{8,10},{9,11},{12,14},{13,15},{16,18},{17,... | collective-permute-start | bytes 2312 | tf_op jit(solution)/shard_map/ppermute | solution.py:24
  74.3 14.4 %collective-permute-start.52 = (f32[3,1,4,130]{3,1,2,0:T(1,128)S(1)}, f32[3,1,4,130]{3,1,2,0:T(1,128)S(1)}, u32[]{:S(2)}, u32[]{:S(2)}) collective-permute-start(f32[3,1,4,130]{3,1,2,0:T(1,128)S(1)} %get-tuple-element.810), channel_id=1, source_target_pairs={{1,0},{3,2},{5,4},{7,6},{9,8},{11,10},{13,12},{15,14},{17,16},{19,... | collective-permute-start | bytes 18728 | tf_op jit(solution)/shard_map/ppermute | solution.py:25
  79.5 15.2 %collective-permute-start.76 = (f32[3,1,4,130]{3,1,2,0:T(1,128)S(1)}, f32[3,1,4,130]{3,1,2,0:T(1,128)S(1)}, u32[]{:S(2)}, u32[]{:S(2)}) collective-permute-start(f32[3,1,4,130]{3,1,2,0:T(1,128)S(1)} %get-tuple-element.814), channel_id=1, source_target_pairs={{1,0},{3,2},{5,4},{7,6},{9,8},{11,10},{13,12},{15,14},{17,16},{19,... | collective-permute-start | bytes 18728 | tf_op jit(solution)/shard_map/ppermute | solution.py:25
  81.0 15.1 %collective-permute-start.77 = (f32[3,1,4,130]{3,1,2,0:T(1,128)S(1)}, f32[3,1,4,130]{3,1,2,0:T(1,128)S(1)}, u32[]{:S(2)}, u32[]{:S(2)}) collective-permute-start(f32[3,1,4,130]{3,1,2,0:T(1,128)S(1)} %get-tuple-element.815), channel_id=1, source_target_pairs={{0,1},{2,3},{4,5},{6,7},{8,9},{10,11},{12,13},{14,15},{16,17},{18,... | collective-permute-start | bytes 18728 | tf_op jit(solution)/shard_map/ppermute | solution.py:24
  84.0 16.7 %collective-permute-start.6 = (f32[3,16,1,128]{3,1,2,0:T(8,128)S(1)}, f32[3,16,1,128]{3,1,2,0:T(8,128)S(1)}, u32[]{:S(2)}, u32[]{:S(2)}) collective-permute-start(f32[3,16,1,128]{3,1,2,0:T(8,128)S(1)} %get-tuple-element.1053), channel_id=1, source_target_pairs={{0,4},{4,8},{8,12},{1,5},{5,9},{9,13},{2,6},{6,10},{10,14},{3,7},{... | collective-permute-start | bytes 73736 | tf_op jit(solution)/shard_map/ppermute | solution.py:24
  90.0 16.7 %collective-permute-start.30 = (f32[3,16,1,128]{3,1,2,0:T(8,128)S(1)}, f32[3,16,1,128]{3,1,2,0:T(8,128)S(1)}, u32[]{:S(2)}, u32[]{:S(2)}) collective-permute-start(f32[3,16,1,128]{3,1,2,0:T(8,128)S(1)} %get-tuple-element.1057), channel_id=1, source_target_pairs={{0,4},{4,8},{8,12},{1,5},{5,9},{9,13},{2,6},{6,10},{10,14},{3,7},{... | collective-permute-start | bytes 73736 | tf_op jit(solution)/shard_map/ppermute | solution.py:24
  111.0 16.7 %collective-permute-start.32 = (f32[3,16,4,1]{3,1,2,0:T(8,128)S(1)}, f32[3,16,4,1]{3,1,2,0:T(8,128)S(1)}, u32[]{:S(2)}, u32[]{:S(2)}) collective-permute-start(f32[3,16,4,1]{3,1,2,0:T(8,128)S(1)} %get-tuple-element.948), channel_id=1, source_target_pairs={{0,2},{1,3},{4,6},{5,7},{8,10},{9,11},{12,14},{13,15},{16,18},{17,... | collective-permute-start | bytes 2312 | tf_op jit(solution)/shard_map/ppermute | solution.py:24
  158.1 15.8 %collective-permute-start.14 = (f32[3,16,128]{2,1,0:T(8,128)S(1)}, f32[3,16,128]{2,1,0:T(8,128)S(1)}, u32[]{:S(2)}, u32[]{:S(2)}) collective-permute-start(f32[3,16,128]{2,1,0:T(8,128)S(1)} %get-tuple-element.797), channel_id=1, source_target_pairs={{4,0},{8,4},{12,8},{5,1},{9,5},{13,9},{6,2},{10,6},{14,10},{7,3},{... | collective-permute-start | bytes 73736 | tf_op jit(solution)/shard_map/ppermute | solution.py:33
  159.4 14.3 %collective-permute-start.12 = (f32[3,2,128]{2,1,0:T(2,128)S(1)}, f32[3,2,128]{2,1,0:T(2,128)S(1)}, u32[]{:S(2)}, u32[]{:S(2)}) collective-permute-start(f32[3,2,128]{2,1,0:T(2,128)S(1)} %bitcast.1244), channel_id=1, source_target_pairs={{1,0},{3,2},{5,4},{7,6},{9,8},{11,10},{13,12},{15,14},{17,16},{19,... | collective-permute-start | bytes 9224 | tf_op jit(solution)/shard_map/ppermute | solution.py:33
  177.0 16.3 %collective-permute-start.18 = (f32[3,2,128]{2,1,0:T(2,128)S(1)}, f32[3,2,128]{2,1,0:T(2,128)S(1)}, u32[]{:S(2)}, u32[]{:S(2)}) collective-permute-start(f32[3,2,128]{2,1,0:T(2,128)S(1)} %bitcast.1241), channel_id=1, source_target_pairs={{1,0},{3,2},{5,4},{7,6},{9,8},{11,10},{13,12},{15,14},{17,16},{19,... | collective-permute-start | bytes 9224 | tf_op jit(solution)/shard_map/ppermute | solution.py:33
  196.4 16.7 %collective-permute-start.36 = (f32[3,2,128]{2,1,0:T(2,128)S(1)}, f32[3,2,128]{2,1,0:T(2,128)S(1)}, u32[]{:S(2)}, u32[]{:S(2)}) collective-permute-start(f32[3,2,128]{2,1,0:T(2,128)S(1)} %bitcast.1268), channel_id=1, source_target_pairs={{1,0},{3,2},{5,4},{7,6},{9,8},{11,10},{13,12},{15,14},{17,16},{19,... | collective-permute-start | bytes 9224 | tf_op jit(solution)/shard_map/ppermute | solution.py:33
  199.3 13.9 %collective-permute-start.37 = (f32[3,2,128]{2,1,0:T(2,128)S(1)}, f32[3,2,128]{2,1,0:T(2,128)S(1)}, u32[]{:S(2)}, u32[]{:S(2)}) collective-permute-start(f32[3,2,128]{2,1,0:T(2,128)S(1)} %bitcast.1271), channel_id=1, source_target_pairs={{0,1},{2,3},{4,5},{6,7},{8,9},{10,11},{12,13},{14,15},{16,17},{18,... | collective-permute-start | bytes 9224 | tf_op jit(solution)/shard_map/ppermute | solution.py:33
  216.3 16.3 %collective-permute-start.42 = (f32[3,2,128]{2,1,0:T(2,128)S(1)}, f32[3,2,128]{2,1,0:T(2,128)S(1)}, u32[]{:S(2)}, u32[]{:S(2)}) collective-permute-start(f32[3,2,128]{2,1,0:T(2,128)S(1)} %bitcast.1242), channel_id=1, source_target_pairs={{1,0},{3,2},{5,4},{7,6},{9,8},{11,10},{13,12},{15,14},{17,16},{19,... | collective-permute-start | bytes 9224 | tf_op jit(solution)/shard_map/ppermute | solution.py:33
  235.7 16.7 %collective-permute-start.60 = (f32[3,2,128]{2,1,0:T(2,128)S(1)}, f32[3,2,128]{2,1,0:T(2,128)S(1)}, u32[]{:S(2)}, u32[]{:S(2)}) collective-permute-start(f32[3,2,128]{2,1,0:T(2,128)S(1)} %bitcast.1269), channel_id=1, source_target_pairs={{1,0},{3,2},{5,4},{7,6},{9,8},{11,10},{13,12},{15,14},{17,16},{19,... | collective-permute-start | bytes 9224 | tf_op jit(solution)/shard_map/ppermute | solution.py:33
  238.6 13.9 %collective-permute-start.61 = (f32[3,2,128]{2,1,0:T(2,128)S(1)}, f32[3,2,128]{2,1,0:T(2,128)S(1)}, u32[]{:S(2)}, u32[]{:S(2)}) collective-permute-start(f32[3,2,128]{2,1,0:T(2,128)S(1)} %bitcast.1272), channel_id=1, source_target_pairs={{0,1},{2,3},{4,5},{6,7},{8,9},{10,11},{12,13},{14,15},{16,17},{18,... | collective-permute-start | bytes 9224 | tf_op jit(solution)/shard_map/ppermute | solution.py:33
  255.5 16.3 %collective-permute-start.66 = (f32[3,2,128]{2,1,0:T(2,128)S(1)}, f32[3,2,128]{2,1,0:T(2,128)S(1)}, u32[]{:S(2)}, u32[]{:S(2)}) collective-permute-start(f32[3,2,128]{2,1,0:T(2,128)S(1)} %bitcast.1243), channel_id=1, source_target_pairs={{1,0},{3,2},{5,4},{7,6},{9,8},{11,10},{13,12},{15,14},{17,16},{19,... | collective-permute-start | bytes 9224 | tf_op jit(solution)/shard_map/ppermute | solution.py:33
  275.0 16.7 %collective-permute-start.84 = (f32[3,2,128]{2,1,0:T(2,128)S(1)}, f32[3,2,128]{2,1,0:T(2,128)S(1)}, u32[]{:S(2)}, u32[]{:S(2)}) collective-permute-start(f32[3,2,128]{2,1,0:T(2,128)S(1)} %bitcast.1270), channel_id=1, source_target_pairs={{1,0},{3,2},{5,4},{7,6},{9,8},{11,10},{13,12},{15,14},{17,16},{19,... | collective-permute-start | bytes 9224 | tf_op jit(solution)/shard_map/ppermute | solution.py:33
  277.9 13.9 %collective-permute-start.85 = (f32[3,2,128]{2,1,0:T(2,128)S(1)}, f32[3,2,128]{2,1,0:T(2,128)S(1)}, u32[]{:S(2)}, u32[]{:S(2)}) collective-permute-start(f32[3,2,128]{2,1,0:T(2,128)S(1)} %bitcast.1273), channel_id=1, source_target_pairs={{0,1},{2,3},{4,5},{6,7},{8,9},{10,11},{12,13},{14,15},{16,17},{18,... | collective-permute-start | bytes 9224 | tf_op jit(solution)/shard_map/ppermute | solution.py:33
  314.3 15.7 %collective-permute-start.90 = (f32[3,2,128]{2,1,0:T(2,128)S(1)}, f32[3,2,128]{2,1,0:T(2,128)S(1)}, u32[]{:S(2)}, u32[]{:S(2)}) collective-permute-start(f32[3,2,128]{2,1,0:T(2,128)S(1)} %bitcast.1236), channel_id=1, source_target_pairs={{1,0},{3,2},{5,4},{7,6},{9,8},{11,10},{13,12},{15,14},{17,16},{19,... | collective-permute-start | bytes 9224 | tf_op jit(solution)/shard_map/ppermute | solution.py:33
  (77 other events, 745.3 us)
